TPU v7x, 32 devices: a whole 2x2x4 slice. The times are simulated.
32 devices in a mesh: groups: 2 (over y), dom: 4 (over z), sub: 2 (over x), field: 2 (over core).
Axes of the slice: x: 2, y: 2, z: 4, core: 2. Of those that a mesh axis runs over, the one named last changes fastest.
Arguments:
- background: float32 [3, 65536], P(None, ('groups', 'dom', 'sub')), parts along dimension 1, may hold values from -6 to 6
- obs_weight: float32 [65536], P(('groups', 'dom', 'sub')), parts along dimension 0, may hold values from 0.02 to 0.2
- connect: int32 [10, 32768], P(None, ('groups', 'dom', 'sub', 'field')), parts along dimension 1, may hold values from 0 to 5631, as said below
- live_blocks: int32 [32], P(('groups', 'dom', 'sub', 'field')), parts along dimension 0, may hold values from 2 to 8, as said below
- elem_scale: float32 [32768], P(('groups', 'dom', 'sub', 'field')), parts along dimension 0, may hold values from 0.5 to 2
- reg_weight: float32 [32768], P(('groups', 'dom', 'sub', 'field')), parts along dimension 0, may hold values from 0.2 to 2
- iterate: float32 [32768], P(('groups', 'dom', 'sub', 'field')), parts along dimension 0, may hold values from -6 to 6
- residual: float32 [32768], P(('groups', 'dom', 'sub', 'field')), parts along dimension 0, may hold values from -30 to 30
- direction: float32 [32768], P(('groups', 'dom', 'sub', 'field')), parts along dimension 0, may hold values from -30 to 30
- send_nodes: int32 [16, 3, 2, 256], P(('groups', 'dom', 'sub')), parts along dimension 0, may hold values from 0 to 4095, as said below
- send_count: int32 [16, 3, 2], P(('groups', 'dom', 'sub')), parts along dimension 0, may hold values from 0 to 256, as said below
- ref_stiff: float32 [30, 30], replicated, may hold values from -1.05 to 4.05, as said below
Outputs:
- iterate_next: float32 [32768], P(('groups', 'dom', 'sub', 'field')), parts along dimension 0
- residual_next: float32 [32768], P(('groups', 'dom', 'sub', 'field')), parts along dimension 0
- direction_next: float32 [32768], P(('groups', 'dom', 'sub', 'field')), parts along dimension 0
There are 2 independent parts, one for each index of `groups`. A program takes and returns all parts, laid end to end along the dimension named above; an argument that names none is the same for every part. Nothing has to cross between parts.
Inputs may be any that keep to these rules, and one draw needn't show every extreme that they name: `send_nodes`: for every link the first send_count slots hold distinct owned nodes; later slots are padding. `send_count`: links go only to partitions of dom index d - 1, d or d + 1 and never to the sender itself or past the ends of dom; some link is full with 256 slots. `connect`: entries from 4096 on name ghost slots that are live slots of their owner's link. `live_blocks`: live blocks fill a device's slots from its first one; some device has 8. `ref_stiff`: Symmetric.
All inputs are finite; a program needn't handle non-finite values.
Results may differ from a plain program's by a relative error of at most 0.00005.
Values sent between devices are 32-bit elements; how exact they have to be, the bound alone decides.
A program may use at most 64 MiB of HBM per device.

v0:
```python
import jax
import jax.numpy as jnp
from jax import lax
from jax.sharding import PartitionSpec as P

BLK = 128


def extended(cells, sides, width):
    for axis, dim in sides:
        count = lax.axis_size(axis)
        ends = count - 1
        head = lax.slice_in_dim(cells, 0, width, axis=dim)
        tail = lax.slice_in_dim(cells, cells.shape[dim] - width, cells.shape[dim], axis=dim)
        cells = jnp.concatenate(
            [
                lax.ppermute(tail, axis, [(i, (i + 1) % count) for i in range(ends)]),
                cells,
                lax.ppermute(head, axis, [((i + 1) % count, i) for i in range(ends)]),
            ],
            axis=dim,
        )
    return cells


def on_device(
    background,
    obs_weight,
    connect,
    live_blocks,
    elem_scale,
    reg_weight,
    iterate,
    residual,
    direction,
    send_nodes,
    send_count,
    ref_stiff,
):
    owned_nodes = background.shape[1]
    sub_count = lax.axis_size("sub")
    link_slots = send_nodes.shape[3]
    element_count = connect.shape[1]
    ghost_slots = 3 * sub_count * link_slots
    targets = send_nodes[0].reshape(-1)
    open_slot = (
        jnp.arange(link_slots, dtype=jnp.int32)[None, None, :] < send_count[0][:, :, None]
    ).astype(jnp.float32)

    def fetch_ghosts(values):
        outbound = values[:, targets].reshape(3, 3, sub_count, link_slots) * open_slot[None]
        mixed = lax.all_to_all(outbound, "sub", split_axis=2, concat_axis=2, tiled=True)
        rimmed = extended(mixed, (("dom", 1),), 1)
        arrived = rimmed[:, 0::2]
        return jnp.concatenate([values, arrived.reshape(3, ghost_slots)], axis=1)

    element = jnp.arange(element_count, dtype=jnp.int32)
    live_mask = (element < BLK * live_blocks[0]).astype(jnp.float32)
    search = live_mask * direction
    remain = live_mask * residual
    guess = live_mask * iterate
    flat_connect = connect.reshape(-1)
    state_full = fetch_ghosts(background)
    element_state = state_full[:, connect].reshape(30, element_count)
    coupled = (live_mask * elem_scale)[None, :] * jnp.dot(
        ref_stiff, element_state, precision=lax.Precision.HIGHEST
    )
    terms = (search[None, :] * coupled).reshape(3, -1)
    accumulated = (
        jnp.zeros((3, owned_nodes + ghost_slots), jnp.float32).at[:, flat_connect].add(terms)
    )
    accumulated = lax.psum(accumulated, "field")
    returning = accumulated[:, owned_nodes:].reshape(3, 3, sub_count, link_slots)
    rimmed = extended(returning, (("dom", 1),), 1)
    landed = lax.all_to_all(rimmed[:, 0::2], "sub", split_axis=2, concat_axis=2, tiled=True)
    landed = (landed * open_slot[None]).reshape(3, -1)
    assembled = accumulated[:, :owned_nodes] + jnp.zeros((3, owned_nodes), jnp.float32).at[
        :, targets
    ].add(landed)
    weighted = obs_weight[None, :] * assembled
    weighted_full = fetch_ghosts(weighted)
    pulled = weighted_full[:, connect].reshape(30, element_count)
    hess_search = jnp.sum(coupled * pulled, axis=0) + reg_weight * search
    squared_before, curvature_sum, cross_term, image_square = lax.psum(
        (
            jnp.sum(remain * remain),
            jnp.sum(search * hess_search),
            jnp.sum(remain * hess_search),
            jnp.sum(hess_search * hess_search),
        ),
        ("dom", "sub", "field"),
    )
    step_length = squared_before / curvature_sum
    iterate_next = guess + step_length * search
    residual_next = remain - step_length * hess_search
    squared_after = (
        squared_before - 2.0 * step_length * cross_term + step_length * step_length * image_square
    )
    direction_next = residual_next + squared_after / squared_before * search
    return (iterate_next, residual_next, direction_next)


def solution(mesh):
    placed = (
        P(None, ("groups", "dom", "sub")),
        P(("groups", "dom", "sub")),
        P(None, ("groups", "dom", "sub", "field")),
        P(("groups", "dom", "sub", "field")),
        P(("groups", "dom", "sub", "field")),
        P(("groups", "dom", "sub", "field")),
        P(("groups", "dom", "sub", "field")),
        P(("groups", "dom", "sub", "field")),
        P(("groups", "dom", "sub", "field")),
        P(("groups", "dom", "sub"), None, None, None),
        P(("groups", "dom", "sub"), None, None),
        P(),
    )
    return jax.shard_map(
        on_device,
        mesh=mesh,
        in_specs=placed,
        out_specs=(
            P(("groups", "dom", "sub", "field")),
            P(("groups", "dom", "sub", "field")),
            P(("groups", "dom", "sub", "field")),
        ),
        check_vma=False,
    )
```

profile of v0, /device:TPU:0, one launch (start us, length us, event | category | flops | bytes accessed | tf_op | source)
XLA Modules:
  0.0 283.6 jit_solution(14023031561616133790)
XLA Ops:
  7.2 0.8 reshape_squeeze.3
  8.0 0.8 fusion.4
  8.8 1.5 copy.66
  10.3 2.6 gather_fusion
  13.8 4.2 %all-to-all-start = ((f32[3,3,2,256]{3,1,0,2:T(4,128)}), f32[3,3,2,256]{3,1,0,2:T(4,128)S(1)}, u32[]{:S(2)}, u32[]{:S(2)}) async-start(f32[3,3,2,256]{3,1,0,2:T(4,128)} %broadcast_multiply_fusion.4), calls=%async_computation | async-start | bytes 49152 | tf_op jit(solution)/shard_map/all_to_all | solution.py:52
  18.9 3.1 %all-to-all-done = f32[3,3,2,256]{3,1,0,2:T(4,128)S(1)} async-done(((f32[3,3,2,256]{3,1,0,2:T(4,128)}), f32[3,3,2,256]{3,1,0,2:T(4,128)S(1)}, u32[]{:S(2)}, u32[]{:S(2)}) %all-to-all-start) | async-done | bytes 18464 | tf_op jit(solution)/shard_map/all_to_all | solution.py:52
  22.0 4.0 %collective-permute-start = (f32[3,1,2,256]{3,1,0,2:T(1,128)S(1)}, f32[3,1,2,256]{3,1,0,2:T(1,128)S(1)}, u32[]{:S(2)}, u32[]{:S(2)}) collective-permute-start(f32[3,1,2,256]{3,1,0,2:T(1,128)S(1)} %get-tuple-element.18), channel_id=1, source_target_pairs={{0,4},{4,8},{8,12},{1,5},{5,9},{9,13},{2,6},{6,10},{10,14},{3,7},{... | collective-permute-start | bytes 18440 | tf_op jit(solution)/shard_map/ppermute | solution.py:17
  25.9 1.3 collective-permute-start.1
  27.3 4.1 %collective-permute-done.1 = f32[3,1,2,256]{3,1,0,2:T(1,128)S(1)} collective-permute-done((f32[3,1,2,256]{3,1,0,2:T(1,128)S(1)}, f32[3,1,2,256]{3,1,0,2:T(1,128)S(1)}, u32[]{:S(2)}, u32[]{:S(2)}) %collective-permute-start.1) | collective-permute-done | bytes 6176 | tf_op jit(solution)/shard_map/ppermute | solution.py:19
  31.6 0.8 copy.71
  32.4 34.2 %gather_fusion.1 = f32[10240,3]{1,0:T(8,128)} fusion(f32[3,5632]{0,1:T(8,128)S(1)} %copy.71, s32[10240]{0:T(1024)S(1)} %broadcast_clamp_fusion), kind=kCustom, calls=%fused_computation.1 | custom fusion | bytes 286720 | tf_op jit(solution)/shard_map/gather | solution.py:64
  66.7 4.2 %copy.72 = f32[10,1024,3]{1,0,2:T(8,128)S(1)} copy(f32[10,1024,3]{2,1,0:T(8,128)} %bitcast.28) | data formatting | bytes 245760 | tf_op jit(solution)/shard_map/gather | solution.py:64
  71.3 3.1 %copy.73 = f32[3,10240]{0,1:T(8,128)} copy(f32[3,10240]{1,0:T(4,128)S(1)} %reshape.145) | data formatting | bytes 245760 | tf_op jit(solution)/shard_map/reshape | solution.py:68
  74.4 51.9 %scatter_custom_fusion = f32[3,5632]{0,1:T(8,128)} fusion(s32[10240]{0:T(1024)S(1)} %bitcast.38, f32[3,10240]{0,1:T(8,128)} %copy.73, f32[]{:T(128)} %constant.7.clone.1), kind=kCustom, calls=%fused_computation.6 | custom fusion | flops 30720 | bytes 190468 | tf_op jit(solution)/shard_map/scatter-add | solution.py:70
  126.3 22.3 %all-reduce.3.cloned.1.call-done = f32[3,5632]{0,1:T(8,128)} async-done(((f32[3,5632]{0,1:T(8,128)}), f32[3,5632]{0,1:T(8,128)}) %all-reduce.3.cloned.1.call-update) | async-done | bytes 67600 | tf_op jit(solution)/shard_map/psum | solution.py:72
  148.6 1.2 slice.55
  150.1 3.8 %collective-permute-start.2 = (f32[3,1,2,256]{3,1,0,2:T(1,128)S(1)}, f32[3,1,2,256]{3,1,0,2:T(1,128)S(1)}, u32[]{:S(2)}, u32[]{:S(2)}) collective-permute-start(f32[3,1,2,256]{3,1,0,2:T(1,128)S(1)} %get-tuple-element.16), channel_id=1, source_target_pairs={{0,4},{4,8},{8,12},{1,5},{5,9},{9,13},{2,6},{6,10},{10,14},{3,7},{... | collective-permute-start | bytes 18440 | tf_op jit(solution)/shard_map/ppermute | solution.py:17
  153.9 1.3 collective-permute-start.3
  155.2 4.2 %collective-permute-done.3 = f32[3,1,2,256]{3,1,0,2:T(1,128)S(1)} collective-permute-done((f32[3,1,2,256]{3,1,0,2:T(1,128)S(1)}, f32[3,1,2,256]{3,1,0,2:T(1,128)S(1)}, u32[]{:S(2)}, u32[]{:S(2)}) %collective-permute-start.3) | collective-permute-done | bytes 6176 | tf_op jit(solution)/shard_map/ppermute | solution.py:19
  160.1 3.2 %all-to-all-start.1 = ((f32[3,3,2,256]{3,1,0,2:T(4,128)}), f32[3,3,2,256]{3,1,0,2:T(4,128)S(1)}, u32[]{:S(2)}, u32[]{:S(2)}) async-start(f32[3,3,2,256]{3,1,0,2:T(4,128)} %slice.40), calls=%async_computation.1 | async-start | bytes 49152 | tf_op jit(solution)/shard_map/all_to_all | solution.py:75
  163.4 3.9 %all-to-all-done.1 = f32[3,3,2,256]{3,1,0,2:T(4,128)S(1)} async-done(((f32[3,3,2,256]{3,1,0,2:T(4,128)}), f32[3,3,2,256]{3,1,0,2:T(4,128)S(1)}, u32[]{:S(2)}, u32[]{:S(2)}) %all-to-all-start.1) | async-done | bytes 18464 | tf_op jit(solution)/shard_map/all_to_all | solution.py:75
  167.6 9.5 %scatter_fusion = f32[3,4096]{0,1:T(8,128)S(1)} fusion(f32[3,4096]{0,1:T(8,128)S(1)} %slice-done, s32[1536]{0:T(1024)S(1)} %fusion.5, f32[1536,3]{1,0:T(8,128)S(1)} %copy.78), kind=kCustom, calls=%fused_computation.5 | custom fusion | flops 4608 | bytes 61440 | tf_op jit(solution)/shard_map/scatter-add | solution.py:79
  177.2 1.9 broadcast_multiply_fusion
  179.1 4.3 %gather_fusion.2 = f32[1536,3]{1,0:T(8,128)S(1)} fusion(f32[3,4096]{0,1:T(8,128)} %broadcast_multiply_fusion, s32[2048]{0:T(1024)S(1)} %pad_clamp_fusion), kind=kCustom, calls=%fused_computation.2 | custom fusion | bytes 43008 | tf_op jit(solution)/shard_map/gather | solution.py:51
  183.8 6.3 %all_to_all.15 = f32[3,3,2,256]{3,1,0,2:T(4,128)S(1)} all-to-all(f32[3,3,2,256]{3,1,0,2:T(4,128)S(1)} %broadcast_multiply_fusion.2), channel_id=1, replica_groups=mesh['groups'=2,'dom'=4,'sub'=2,'field'=2] {'sub'}, dimensions={2} | all-to-all | bytes 36864 | tf_op jit(solution)/shard_map/all_to_all | solution.py:52
  190.1 3.4 %collective-permute-start.4 = (f32[3,1,2,256]{3,1,0,2:T(1,128)S(1)}, f32[3,1,2,256]{3,1,0,2:T(1,128)S(1)}, u32[]{:S(2)}, u32[]{:S(2)}) collective-permute-start(f32[3,1,2,256]{3,1,0,2:T(1,128)S(1)} %get-tuple-element.14), channel_id=1, source_target_pairs={{0,4},{4,8},{8,12},{1,5},{5,9},{9,13},{2,6},{6,10},{10,14},{3,7},{... | collective-permute-start | bytes 18440 | tf_op jit(solution)/shard_map/ppermute | solution.py:17
  193.5 1.3 collective-permute-start.5
  194.8 4.2 %collective-permute-done.5 = f32[3,1,2,256]{3,1,0,2:T(1,128)S(1)} collective-permute-done((f32[3,1,2,256]{3,1,0,2:T(1,128)S(1)}, f32[3,1,2,256]{3,1,0,2:T(1,128)S(1)}, u32[]{:S(2)}, u32[]{:S(2)}) %collective-permute-start.5) | collective-permute-done | bytes 6176 | tf_op jit(solution)/shard_map/ppermute | solution.py:19
  199.3 1.7 pad_maximum_fusion
  201.1 36.1 %gather_fusion.3 = f32[10240,3]{1,0:T(8,128)} fusion(f32[3,5632]{0,1:T(8,128)} %pad_maximum_fusion, s32[10240]{0:T(1024)S(1)} %broadcast_clamp_fusion), kind=kCustom, calls=%fused_computation.3 | custom fusion | bytes 286720 | tf_op jit(solution)/shard_map/gather | solution.py:82
  237.1 4.2 %copy.84 = f32[10,1024,3]{1,0,2:T(8,128)S(1)} copy(f32[10,1024,3]{2,1,0:T(8,128)} %bitcast.27) | data formatting | bytes 245760 | tf_op jit(solution)/shard_map/gather | solution.py:82
  242.1 30.1 %all-reduce = (f32[]{:T(128)}, f32[]{:T(128)}, f32[]{:T(128)}, f32[]{:T(128)}) all-reduce(f32[]{:T(128)} %get-tuple-element.5, f32[]{:T(128)} %get-tuple-element.6, f32[]{:T(128)} %get-tuple-element.4, f32[]{:T(128)} %get-tuple-element.3), channel_id=1, replica_groups=mesh['groups'=2,'dom'=4,'sub'=2,'field'=2] {'dom','sub','field'}, use_global_device_ids=true, to_apply=%region_1.0 | all-reduce | flops 4 | bytes 32 | tf_op jit(solution)/shard_map/psum | solution.py:84
  (69 shorter events, 5.0 us)
Async XLA Ops:
  7.2 63.7 %copy-start = (f32[30,30]{1,0:T(8,128)S(1)}, f32[30,30]{1,0:T(8,128)}, u32[]{:S(2)}) copy-start(f32[30,30]{1,0:T(8,128)} %param.23) | copy-start | bytes 10804
  7.2 24.4 %copy-start.2 = (f32[3,4096]{1,0:T(4,128)S(1)}, f32[3,4096]{1,0:T(4,128)}, u32[]{:S(2)}) copy-start(f32[3,4096]{1,0:T(4,128)} %param.12) | copy-start | bytes 147460
  7.2 10.9 %copy-start.3 = (s32[10,1024]{1,0:T(8,128)S(1)}, s32[10,1024]{1,0:T(8,128)}, u32[]{:S(2)}) copy-start(s32[10,1024]{1,0:T(8,128)} %param.14) | copy-start | bytes 122884
  7.2 20.0 %copy-start.7 = (f32[1024]{0:T(1024)S(1)}, f32[1024]{0:T(1024)}, u32[]{:S(2)}) copy-start(f32[1024]{0:T(1024)} %param.20) | copy-start | bytes 12292
  7.2 20.0 %copy-start.6 = (f32[1024]{0:T(1024)S(1)}, f32[1024]{0:T(1024)}, u32[]{:S(2)}) copy-start(f32[1024]{0:T(1024)} %param.16) | copy-start | bytes 12292
  13.8 8.1 %all-to-all-start = ((f32[3,3,2,256]{3,1,0,2:T(4,128)}), f32[3,3,2,256]{3,1,0,2:T(4,128)S(1)}, u32[]{:S(2)}, u32[]{:S(2)}) async-start(f32[3,3,2,256]{3,1,0,2:T(4,128)} %broadcast_multiply_fusion.4), calls=%async_computation | async-start | bytes 49152 | tf_op jit(solution)/shard_map/all_to_all | solution.py:52
  18.1 130.5 %all-reduce.3.cloned.1.call-start = ((), (), s32[]{:S(2)}) async-start(), calls=%async_computation.3 | async-start | bytes 5767168 | tf_op jit(solution)/shard_map/psum | solution.py:72
  22.0 5.3 %collective-permute-start = (f32[3,1,2,256]{3,1,0,2:T(1,128)S(1)}, f32[3,1,2,256]{3,1,0,2:T(1,128)S(1)}, u32[]{:S(2)}, u32[]{:S(2)}) collective-permute-start(f32[3,1,2,256]{3,1,0,2:T(1,128)S(1)} %get-tuple-element.18), channel_id=1, source_target_pairs={{0,4},{4,8},{8,12},{1,5},{5,9},{9,13},{2,6},{6,10},{10,14},{3,7},{... | collective-permute-start | bytes 18440 | tf_op jit(solution)/shard_map/ppermute | solution.py:17
  25.9 5.5 %collective-permute-start.1 = (f32[3,1,2,256]{3,1,0,2:T(1,128)S(1)}, f32[3,1,2,256]{3,1,0,2:T(1,128)S(1)}, u32[]{:S(2)}, u32[]{:S(2)}) collective-permute-start(f32[3,1,2,256]{3,1,0,2:T(1,128)S(1)} %get-tuple-element.19), channel_id=1, source_target_pairs={{4,0},{8,4},{12,8},{5,1},{9,5},{13,9},{6,2},{10,6},{14,10},{7,3},{... | collective-permute-start | bytes 18440 | tf_op jit(solution)/shard_map/ppermute | solution.py:19
  150.1 17.5 %slice-start = ((f32[3,5632]{0,1:T(8,128)}), f32[3,4096]{0,1:T(8,128)S(1)}, s32[]{:S(2)}) async-start(f32[3,5632]{0,1:T(8,128)} %all-reduce.3.cloned.1.call-done), calls=%async_computation.4 | async-start | bytes 4194304 | tf_op jit(solution)/shard_map/slice | solution.py:77
  150.1 27.0 %copy-start.4 = (f32[4096]{0:T(1024)S(1)}, f32[4096]{0:T(1024)}, u32[]{:S(2)}) copy-start(f32[4096]{0:T(1024)} %param.13) | copy-start | bytes 49156
  150.1 5.1 %collective-permute-start.2 = (f32[3,1,2,256]{3,1,0,2:T(1,128)S(1)}, f32[3,1,2,256]{3,1,0,2:T(1,128)S(1)}, u32[]{:S(2)}, u32[]{:S(2)}) collective-permute-start(f32[3,1,2,256]{3,1,0,2:T(1,128)S(1)} %get-tuple-element.16), channel_id=1, source_target_pairs={{0,4},{4,8},{8,12},{1,5},{5,9},{9,13},{2,6},{6,10},{10,14},{3,7},{... | collective-permute-start | bytes 18440 | tf_op jit(solution)/shard_map/ppermute | solution.py:17
  153.9 5.5 %collective-permute-start.3 = (f32[3,1,2,256]{3,1,0,2:T(1,128)S(1)}, f32[3,1,2,256]{3,1,0,2:T(1,128)S(1)}, u32[]{:S(2)}, u32[]{:S(2)}) collective-permute-start(f32[3,1,2,256]{3,1,0,2:T(1,128)S(1)} %get-tuple-element.17), channel_id=1, source_target_pairs={{4,0},{8,4},{12,8},{5,1},{9,5},{13,9},{6,2},{10,6},{14,10},{7,3},{... | collective-permute-start | bytes 18440 | tf_op jit(solution)/shard_map/ppermute | solution.py:19
  160.1 7.1 %all-to-all-start.1 = ((f32[3,3,2,256]{3,1,0,2:T(4,128)}), f32[3,3,2,256]{3,1,0,2:T(4,128)S(1)}, u32[]{:S(2)}, u32[]{:S(2)}) async-start(f32[3,3,2,256]{3,1,0,2:T(4,128)} %slice.40), calls=%async_computation.1 | async-start | bytes 49152 | tf_op jit(solution)/shard_map/all_to_all | solution.py:75
  179.1 20.2 %copy-start.1 = (f32[3,4096]{0,1:T(8,128)S(1)}, f32[3,4096]{0,1:T(8,128)}, u32[]{:S(2)}) copy-start(f32[3,4096]{0,1:T(8,128)} %broadcast_multiply_fusion) | copy-start | bytes 147460
  190.1 4.7 %collective-permute-start.4 = (f32[3,1,2,256]{3,1,0,2:T(1,128)S(1)}, f32[3,1,2,256]{3,1,0,2:T(1,128)S(1)}, u32[]{:S(2)}, u32[]{:S(2)}) collective-permute-start(f32[3,1,2,256]{3,1,0,2:T(1,128)S(1)} %get-tuple-element.14), channel_id=1, source_target_pairs={{0,4},{4,8},{8,12},{1,5},{5,9},{9,13},{2,6},{6,10},{10,14},{3,7},{... | collective-permute-start | bytes 18440 | tf_op jit(solution)/shard_map/ppermute | solution.py:17
  193.5 5.5 %collective-permute-start.5 = (f32[3,1,2,256]{3,1,0,2:T(1,128)S(1)}, f32[3,1,2,256]{3,1,0,2:T(1,128)S(1)}, u32[]{:S(2)}, u32[]{:S(2)}) collective-permute-start(f32[3,1,2,256]{3,1,0,2:T(1,128)S(1)} %get-tuple-element.15), channel_id=1, source_target_pairs={{4,0},{8,4},{12,8},{5,1},{9,5},{13,9},{6,2},{10,6},{14,10},{7,3},{... | collective-permute-start | bytes 18440 | tf_op jit(solution)/shard_map/ppermute | solution.py:19
  237.1 4.3 %copy-start.5 = (f32[1024]{0:T(1024)S(1)}, f32[1024]{0:T(1024)}, u32[]{:S(2)}) copy-start(f32[1024]{0:T(1024)} %param.19) | copy-start | bytes 12292
  237.1 4.3 %copy-start.8 = (f32[1024]{0:T(1024)S(1)}, f32[1024]{0:T(1024)}, u32[]{:S(2)}) copy-start(f32[1024]{0:T(1024)} %param.17) | copy-start | bytes 12292
  237.1 39.0 %copy-start.9 = (f32[1024]{0:T(1024)S(1)}, f32[1024]{0:T(1024)}, u32[]{:S(2)}) copy-start(f32[1024]{0:T(1024)} %param.18) | copy-start | bytes 12292
Sparse Core Ops, SparseCore 0:
  126.4 22.0 all-reduce.2
where the time goes:
time: 284 us
  local copies, waits for them, and re-layouts  95.7 us (34%)
  other arithmetic  67.9 us (24%)
  waiting for transfers between devices  41.8 us (15%)
  blocking collectives  36.4 us (13%)
  starting transfers between devices  22.5 us (8%)
  between operations  19.1 us (7%)
    scatter-add x1, other arithmetic, on_device(): jnp.zeros((3, owned_nodes + ghost_slots), jnp.float32).at[:, flat_connect]  51.9 us
    gather x2, local copies, waits for them, and re-layouts, on_device(): pulled = weighted_full[:, connect].reshape(30, element_count)  40.3 us
    gather x2, local copies, waits for them, and re-layouts, on_device(): element_state = state_full[:, connect].reshape(30, element_count)  38.4 us
    psum x1, blocking collectives, on_device(): lax.psum((jnp.sum(remain * remain), jnp.sum(search * hess_search), jnp.su...  30.1 us
    psum x1, waiting for transfers between devices, on_device(): accumulated = lax.psum(accumulated, 'field')  22.3 us
    ppermute x3, waiting for transfers between devices, extended(): lax.ppermute(head, axis, [((i + 1) % count, i) for i in range(ends)])  12.5 us
    ppermute x3, starting transfers between devices, extended(): lax.ppermute(tail, axis, [(i, (i + 1) % count) for i in range(ends)])  11.1 us
    scatter-add x1, other arithmetic, on_device(): assembled = accumulated[:, :owned_nodes] + jnp.zeros((3, owned_nodes), jn...  9.52 us
  transfers between devices with their start and end apart: 9, of which 6 were waited for; matrix products, arithmetic and copies ran while one was open for 0% of the time, Pallas kernels for 0%

commit v1 on v0

--- a/solution.py
+++ b/solution.py
@@ -69,7 +69,7 @@
     accumulated = (
         jnp.zeros((3, owned_nodes + ghost_slots), jnp.float32).at[:, flat_connect].add(terms)
     )
-    accumulated = lax.psum(accumulated, "field")
+    accumulated = jnp.sum(lax.all_gather(accumulated, "field"), axis=0)
     returning = accumulated[:, owned_nodes:].reshape(3, 3, sub_count, link_slots)
     rimmed = extended(returning, (("dom", 1),), 1)
     landed = lax.all_to_all(rimmed[:, 0::2], "sub", split_axis=2, concat_axis=2, tiled=True)

time: 284 us -> 249 us (0.88)
  waiting for transfers between devices: 41.8 us -> 18.9 us
  between operations: 19.1 us -> 5.65 us
    psum x1 -> x0, waiting for transfers between devices: 22.3 us -> none  [on_device(): accumulated = lax.psum(accumulated, 'field')]
  transfers between devices with their start and end apart: 9 -> 8, of which waited for: 6 -> 5; matrix products, arithmetic and copies ran while one was open for 0% -> 0% of each run, Pallas kernels for 0% -> 0%
where the time goes in v1:
time: 249 us; the launch traced here: 248 us
  local copies, waits for them, and re-layouts  95.7 us (38%)
  other arithmetic  67.1 us (27%)
  blocking collectives  38.4 us (15%)
  starting transfers between devices  22.3 us (9%)
  waiting for transfers between devices  18.9 us (8%)
  between operations  5.65 us (2%)
    scatter-add x1, other arithmetic, on_device(): jnp.zeros((3, owned_nodes + ghost_slots), jnp.float32).at[:, flat_connect]  50.9 us
    gather x2, local copies, waits for them, and re-layouts, on_device(): pulled = weighted_full[:, connect].reshape(30, element_count)  40.3 us
    gather x2, local copies, waits for them, and re-layouts, on_device(): element_state = state_full[:, connect].reshape(30, element_count)  38.5 us
    psum x1, blocking collectives, on_device(): lax.psum((jnp.sum(remain * remain), jnp.sum(search * hess_search), jnp.su...  30.1 us
    ppermute x3, waiting for transfers between devices, extended(): lax.ppermute(head, axis, [((i + 1) % count, i) for i in range(ends)])  12.5 us
    ppermute x3, starting transfers between devices, extended(): lax.ppermute(tail, axis, [(i, (i + 1) % count) for i in range(ends)])  10.9 us
    scatter-add x1, other arithmetic, on_device(): assembled = accumulated[:, :owned_nodes] + jnp.zeros((3, owned_nodes), jn...  9.52 us
    gather x2, local copies, waits for them, and re-layouts, fetch_ghosts(): values[:, targets].reshape(3, 3, sub_count, link_slots) * open_slot[None]  6.92 us
  transfers between devices with their start and end apart: 8, of which 5 were waited for; matrix products, arithmetic and copies ran while one was open for 0% of the time, Pallas kernels for 0%

profile of v1, /device:TPU:0, one launch (start us, length us, event | category | flops | bytes accessed | tf_op | source)
XLA Modules:
  0.0 248.2 jit_solution(15532677477096466108)
XLA Ops:
  0.7 0.8 reshape_squeeze.3
  1.5 0.8 fusion.4
  2.3 1.5 copy.88
  3.7 2.6 %gather_fusion = f32[1536,3]{1,0:T(8,128)S(1)} fusion(f32[3,4096]{0,1:T(8,128)S(1)} %copy.88, s32[2048]{0:T(1024)S(1)} %pad_clamp_fusion), kind=kCustom, calls=%fused_computation | custom fusion | bytes 43008 | tf_op jit(solution)/shard_map/gather | solution.py:51
  7.3 4.2 %all-to-all-start = ((f32[3,3,2,256]{3,1,0,2:T(4,128)}), f32[3,3,2,256]{3,1,0,2:T(4,128)S(1)}, u32[]{:S(2)}, u32[]{:S(2)}) async-start(f32[3,3,2,256]{3,1,0,2:T(4,128)} %broadcast_multiply_fusion.4), calls=%async_computation | async-start | bytes 49152 | tf_op jit(solution)/shard_map/all_to_all | solution.py:52
  12.3 3.1 %all-to-all-done = f32[3,3,2,256]{3,1,0,2:T(4,128)S(1)} async-done(((f32[3,3,2,256]{3,1,0,2:T(4,128)}), f32[3,3,2,256]{3,1,0,2:T(4,128)S(1)}, u32[]{:S(2)}, u32[]{:S(2)}) %all-to-all-start) | async-done | bytes 18464 | tf_op jit(solution)/shard_map/all_to_all | solution.py:52
  15.4 4.0 %collective-permute-start = (f32[3,1,2,256]{3,1,0,2:T(1,128)S(1)}, f32[3,1,2,256]{3,1,0,2:T(1,128)S(1)}, u32[]{:S(2)}, u32[]{:S(2)}) collective-permute-start(f32[3,1,2,256]{3,1,0,2:T(1,128)S(1)} %get-tuple-element.16), channel_id=1, source_target_pairs={{0,4},{4,8},{8,12},{1,5},{5,9},{9,13},{2,6},{6,10},{10,14},{3,7},{... | collective-permute-start | bytes 18440 | tf_op jit(solution)/shard_map/ppermute | solution.py:17
  19.4 1.3 collective-permute-start.1
  20.8 4.1 %collective-permute-done.1 = f32[3,1,2,256]{3,1,0,2:T(1,128)S(1)} collective-permute-done((f32[3,1,2,256]{3,1,0,2:T(1,128)S(1)}, f32[3,1,2,256]{3,1,0,2:T(1,128)S(1)}, u32[]{:S(2)}, u32[]{:S(2)}) %collective-permute-start.1) | collective-permute-done | bytes 6176 | tf_op jit(solution)/shard_map/ppermute | solution.py:19
  25.0 0.8 copy.93
  25.9 34.3 %gather_fusion.1 = f32[10240,3]{1,0:T(8,128)} fusion(f32[3,5632]{0,1:T(8,128)S(1)} %copy.93, s32[10240]{0:T(1024)S(1)} %broadcast_clamp_fusion), kind=kCustom, calls=%fused_computation.1 | custom fusion | bytes 286720 | tf_op jit(solution)/shard_map/gather | solution.py:64
  60.2 4.2 %copy.94 = f32[10,1024,3]{1,0,2:T(8,128)S(1)} copy(f32[10,1024,3]{2,1,0:T(8,128)} %bitcast.29) | data formatting | bytes 245760 | tf_op jit(solution)/shard_map/gather | solution.py:64
  64.8 3.1 %copy.95 = f32[3,10240]{0,1:T(8,128)} copy(f32[3,10240]{1,0:T(4,128)S(1)} %reshape.145) | data formatting | bytes 245760 | tf_op jit(solution)/shard_map/reshape | solution.py:68
  67.9 50.9 %scatter_custom_fusion = f32[3,5632]{0,1:T(8,128)S(1)} fusion(s32[10240]{0:T(1024)S(1)} %bitcast.38, f32[3,10240]{0,1:T(8,128)} %copy.95, f32[]{:T(128)} %constant.7.clone.1), kind=kCustom, calls=%fused_computation.6 | custom fusion | flops 30720 | bytes 190468 | tf_op jit(solution)/shard_map/scatter-add | solution.py:70
  118.8 0.8 copy.96
  119.6 2.1 all-gather.1
  121.8 3.5 %collective-permute-start.2 = (f32[3,1,2,256]{3,2,1,0:T(2,128)S(1)}, f32[3,1,2,256]{3,2,1,0:T(2,128)S(1)}, u32[]{:S(2)}, u32[]{:S(2)}) collective-permute-start(f32[3,1,2,256]{3,2,1,0:T(2,128)S(1)} %get-tuple-element.18), channel_id=1, source_target_pairs={{0,4},{4,8},{8,12},{1,5},{5,9},{9,13},{2,6},{6,10},{10,14},{3,7},{... | collective-permute-start | bytes 18440 | tf_op jit(solution)/shard_map/ppermute | solution.py:17
  125.3 1.3 collective-permute-start.3
  126.6 4.2 %collective-permute-done.3 = f32[3,1,2,256]{3,2,1,0:T(2,128)S(1)} collective-permute-done((f32[3,1,2,256]{3,2,1,0:T(2,128)S(1)}, f32[3,1,2,256]{3,2,1,0:T(2,128)S(1)}, u32[]{:S(2)}, u32[]{:S(2)}) %collective-permute-start.3) | collective-permute-done | bytes 6176 | tf_op jit(solution)/shard_map/ppermute | solution.py:19
  131.5 3.2 %all-to-all-start.1 = ((f32[3,3,2,256]{3,1,0,2:T(4,128)}), f32[3,3,2,256]{3,1,0,2:T(4,128)S(1)}, u32[]{:S(2)}, u32[]{:S(2)}) async-start(f32[3,3,2,256]{3,1,0,2:T(4,128)} %copy.107), calls=%async_computation.1 | async-start | bytes 49152 | tf_op jit(solution)/shard_map/all_to_all | solution.py:75
  135.4 3.2 %all-to-all-done.1 = f32[3,3,2,256]{3,1,0,2:T(4,128)S(1)} async-done(((f32[3,3,2,256]{3,1,0,2:T(4,128)}), f32[3,3,2,256]{3,1,0,2:T(4,128)S(1)}, u32[]{:S(2)}, u32[]{:S(2)}) %all-to-all-start.1) | async-done | bytes 18464 | tf_op jit(solution)/shard_map/all_to_all | solution.py:75
  139.0 9.5 %scatter_fusion = f32[3,4096]{0,1:T(8,128)S(1)} fusion(f32[3,4096]{0,1:T(8,128)S(1)} %copy.99, s32[1536]{0:T(1024)S(1)} %fusion.5, f32[1536,3]{1,0:T(8,128)S(1)} %copy.100), kind=kCustom, calls=%fused_computation.5 | custom fusion | flops 4608 | bytes 61440 | tf_op jit(solution)/shard_map/scatter-add | solution.py:79
  148.5 2.0 broadcast_multiply_fusion
  150.5 4.3 %gather_fusion.2 = f32[1536,3]{1,0:T(8,128)S(1)} fusion(f32[3,4096]{0,1:T(8,128)} %broadcast_multiply_fusion, s32[2048]{0:T(1024)S(1)} %pad_clamp_fusion), kind=kCustom, calls=%fused_computation.2 | custom fusion | bytes 43008 | tf_op jit(solution)/shard_map/gather | solution.py:51
  155.1 6.3 %all_to_all.15 = f32[3,3,2,256]{3,1,0,2:T(4,128)S(1)} all-to-all(f32[3,3,2,256]{3,1,0,2:T(4,128)S(1)} %broadcast_multiply_fusion.2), channel_id=1, replica_groups=mesh['groups'=2,'dom'=4,'sub'=2,'field'=2] {'sub'}, dimensions={2} | all-to-all | bytes 36864 | tf_op jit(solution)/shard_map/all_to_all | solution.py:52
  161.4 3.5 %collective-permute-start.4 = (f32[3,1,2,256]{3,1,0,2:T(1,128)S(1)}, f32[3,1,2,256]{3,1,0,2:T(1,128)S(1)}, u32[]{:S(2)}, u32[]{:S(2)}) collective-permute-start(f32[3,1,2,256]{3,1,0,2:T(1,128)S(1)} %get-tuple-element.14), channel_id=1, source_target_pairs={{0,4},{4,8},{8,12},{1,5},{5,9},{9,13},{2,6},{6,10},{10,14},{3,7},{... | collective-permute-start | bytes 18440 | tf_op jit(solution)/shard_map/ppermute | solution.py:17
  164.9 1.3 collective-permute-start.5
  166.3 4.2 %collective-permute-done.5 = f32[3,1,2,256]{3,1,0,2:T(1,128)S(1)} collective-permute-done((f32[3,1,2,256]{3,1,0,2:T(1,128)S(1)}, f32[3,1,2,256]{3,1,0,2:T(1,128)S(1)}, u32[]{:S(2)}, u32[]{:S(2)}) %collective-permute-start.5) | collective-permute-done | bytes 6176 | tf_op jit(solution)/shard_map/ppermute | solution.py:19
  170.8 1.7 pad_maximum_fusion
  172.5 36.1 %gather_fusion.3 = f32[10240,3]{1,0:T(8,128)} fusion(f32[3,5632]{0,1:T(8,128)} %pad_maximum_fusion, s32[10240]{0:T(1024)S(1)} %broadcast_clamp_fusion), kind=kCustom, calls=%fused_computation.3 | custom fusion | bytes 286720 | tf_op jit(solution)/shard_map/gather | solution.py:82
  208.6 4.2 %copy.106 = f32[10,1024,3]{1,0,2:T(8,128)S(1)} copy(f32[10,1024,3]{2,1,0:T(8,128)} %bitcast.28) | data formatting | bytes 245760 | tf_op jit(solution)/shard_map/gather | solution.py:82
  213.6 30.1 %all-reduce = (f32[]{:T(128)}, f32[]{:T(128)}, f32[]{:T(128)}, f32[]{:T(128)}) all-reduce(f32[]{:T(128)} %get-tuple-element.5, f32[]{:T(128)} %get-tuple-element.6, f32[]{:T(128)} %get-tuple-element.4, f32[]{:T(128)} %get-tuple-element.3), channel_id=1, replica_groups=mesh['groups'=2,'dom'=4,'sub'=2,'field'=2] {'dom','sub','field'}, use_global_device_ids=true, to_apply=%region_1.0 | all-reduce | flops 4 | bytes 32 | tf_op jit(solution)/shard_map/psum | solution.py:84
  (70 shorter events, 5.4 us)
Async XLA Ops:
  0.6 63.8 %copy-start = (f32[30,30]{1,0:T(8,128)S(1)}, f32[30,30]{1,0:T(8,128)}, u32[]{:S(2)}) copy-start(f32[30,30]{1,0:T(8,128)} %param.23) | copy-start | bytes 10804
  0.6 24.3 %copy-start.2 = (f32[3,4096]{1,0:T(4,128)S(1)}, f32[3,4096]{1,0:T(4,128)}, u32[]{:S(2)}) copy-start(f32[3,4096]{1,0:T(4,128)} %param.12) | copy-start | bytes 147460
  0.7 10.9 %copy-start.3 = (s32[10,1024]{1,0:T(8,128)S(1)}, s32[10,1024]{1,0:T(8,128)}, u32[]{:S(2)}) copy-start(s32[10,1024]{1,0:T(8,128)} %param.14) | copy-start | bytes 122884
  0.7 20.0 %copy-start.7 = (f32[1024]{0:T(1024)S(1)}, f32[1024]{0:T(1024)}, u32[]{:S(2)}) copy-start(f32[1024]{0:T(1024)} %param.20) | copy-start | bytes 12292
  0.7 20.0 %copy-start.6 = (f32[1024]{0:T(1024)S(1)}, f32[1024]{0:T(1024)}, u32[]{:S(2)}) copy-start(f32[1024]{0:T(1024)} %param.16) | copy-start | bytes 12292
  7.3 8.1 %all-to-all-start = ((f32[3,3,2,256]{3,1,0,2:T(4,128)}), f32[3,3,2,256]{3,1,0,2:T(4,128)S(1)}, u32[]{:S(2)}, u32[]{:S(2)}) async-start(f32[3,3,2,256]{3,1,0,2:T(4,128)} %broadcast_multiply_fusion.4), calls=%async_computation | async-start | bytes 49152 | tf_op jit(solution)/shard_map/all_to_all | solution.py:52
  15.4 5.3 %collective-permute-start = (f32[3,1,2,256]{3,1,0,2:T(1,128)S(1)}, f32[3,1,2,256]{3,1,0,2:T(1,128)S(1)}, u32[]{:S(2)}, u32[]{:S(2)}) collective-permute-start(f32[3,1,2,256]{3,1,0,2:T(1,128)S(1)} %get-tuple-element.16), channel_id=1, source_target_pairs={{0,4},{4,8},{8,12},{1,5},{5,9},{9,13},{2,6},{6,10},{10,14},{3,7},{... | collective-permute-start | bytes 18440 | tf_op jit(solution)/shard_map/ppermute | solution.py:17
  19.4 5.5 %collective-permute-start.1 = (f32[3,1,2,256]{3,1,0,2:T(1,128)S(1)}, f32[3,1,2,256]{3,1,0,2:T(1,128)S(1)}, u32[]{:S(2)}, u32[]{:S(2)}) collective-permute-start(f32[3,1,2,256]{3,1,0,2:T(1,128)S(1)} %get-tuple-element.17), channel_id=1, source_target_pairs={{4,0},{8,4},{12,8},{5,1},{9,5},{13,9},{6,2},{10,6},{14,10},{7,3},{... | collective-permute-start | bytes 18440 | tf_op jit(solution)/shard_map/ppermute | solution.py:19
  119.6 28.8 %copy-start.4 = (f32[4096]{0:T(1024)S(1)}, f32[4096]{0:T(1024)}, u32[]{:S(2)}) copy-start(f32[4096]{0:T(1024)} %param.13) | copy-start | bytes 49156
  121.8 4.8 %collective-permute-start.2 = (f32[3,1,2,256]{3,2,1,0:T(2,128)S(1)}, f32[3,1,2,256]{3,2,1,0:T(2,128)S(1)}, u32[]{:S(2)}, u32[]{:S(2)}) collective-permute-start(f32[3,1,2,256]{3,2,1,0:T(2,128)S(1)} %get-tuple-element.18), channel_id=1, source_target_pairs={{0,4},{4,8},{8,12},{1,5},{5,9},{9,13},{2,6},{6,10},{10,14},{3,7},{... | collective-permute-start | bytes 18440 | tf_op jit(solution)/shard_map/ppermute | solution.py:17
  125.3 5.5 %collective-permute-start.3 = (f32[3,1,2,256]{3,2,1,0:T(2,128)S(1)}, f32[3,1,2,256]{3,2,1,0:T(2,128)S(1)}, u32[]{:S(2)}, u32[]{:S(2)}) collective-permute-start(f32[3,1,2,256]{3,2,1,0:T(2,128)S(1)} %get-tuple-element.19), channel_id=1, source_target_pairs={{4,0},{8,4},{12,8},{5,1},{9,5},{13,9},{6,2},{10,6},{14,10},{7,3},{... | collective-permute-start | bytes 18440 | tf_op jit(solution)/shard_map/ppermute | solution.py:19
  131.5 7.1 %all-to-all-start.1 = ((f32[3,3,2,256]{3,1,0,2:T(4,128)}), f32[3,3,2,256]{3,1,0,2:T(4,128)S(1)}, u32[]{:S(2)}, u32[]{:S(2)}) async-start(f32[3,3,2,256]{3,1,0,2:T(4,128)} %copy.107), calls=%async_computation.1 | async-start | bytes 49152 | tf_op jit(solution)/shard_map/all_to_all | solution.py:75
  150.5 20.3 %copy-start.1 = (f32[3,4096]{0,1:T(8,128)S(1)}, f32[3,4096]{0,1:T(8,128)}, u32[]{:S(2)}) copy-start(f32[3,4096]{0,1:T(8,128)} %broadcast_multiply_fusion) | copy-start | bytes 147460
  161.4 4.8 %collective-permute-start.4 = (f32[3,1,2,256]{3,1,0,2:T(1,128)S(1)}, f32[3,1,2,256]{3,1,0,2:T(1,128)S(1)}, u32[]{:S(2)}, u32[]{:S(2)}) collective-permute-start(f32[3,1,2,256]{3,1,0,2:T(1,128)S(1)} %get-tuple-element.14), channel_id=1, source_target_pairs={{0,4},{4,8},{8,12},{1,5},{5,9},{9,13},{2,6},{6,10},{10,14},{3,7},{... | collective-permute-start | bytes 18440 | tf_op jit(solution)/shard_map/ppermute | solution.py:17
  164.9 5.5 %collective-permute-start.5 = (f32[3,1,2,256]{3,1,0,2:T(1,128)S(1)}, f32[3,1,2,256]{3,1,0,2:T(1,128)S(1)}, u32[]{:S(2)}, u32[]{:S(2)}) collective-permute-start(f32[3,1,2,256]{3,1,0,2:T(1,128)S(1)} %get-tuple-element.15), channel_id=1, source_target_pairs={{4,0},{8,4},{12,8},{5,1},{9,5},{13,9},{6,2},{10,6},{14,10},{7,3},{... | collective-permute-start | bytes 18440 | tf_op jit(solution)/shard_map/ppermute | solution.py:19
  208.6 4.3 %copy-start.5 = (f32[1024]{0:T(1024)S(1)}, f32[1024]{0:T(1024)}, u32[]{:S(2)}) copy-start(f32[1024]{0:T(1024)} %param.19) | copy-start | bytes 12292
  208.6 4.3 %copy-start.8 = (f32[1024]{0:T(1024)S(1)}, f32[1024]{0:T(1024)}, u32[]{:S(2)}) copy-start(f32[1024]{0:T(1024)} %param.17) | copy-start | bytes 12292
  208.6 39.0 %copy-start.9 = (f32[1024]{0:T(1024)S(1)}, f32[1024]{0:T(1024)}, u32[]{:S(2)}) copy-start(f32[1024]{0:T(1024)} %param.18) | copy-start | bytes 12292
